TPU v7x, 128 devices: a whole 4x4x4 slice. The times are simulated.
128 devices in a mesh: bx: 8 (over y, x_hi), by: 16 (over x_lo, z, core).
Axes of the slice: x: 4 (x_hi: 2, x_lo: 2; x = x_hi * 2 + x_lo), y: 4, z: 4, core: 2. Of those that a mesh axis runs over, the one named last changes fastest.
Arguments:
- speed_vectors: float32 [3, 6, 120, 240, 128], P(None, None, 'bx', 'by'), may hold values from -10 to 10, as said below
- bin_population: int32 [120, 240, 128], P('bx', 'by'), may hold values from 0 to 6, as said below
- spin_choice: int32 [12, 120, 240, 128], P(None, 'bx', 'by'), may hold values from 0 to 5
- approval_flags: int32 [12, 120, 240, 128], P(None, 'bx', 'by'), may hold values 0 or 1
- round_evenness: int32 [12], replicated, may hold values from 0 to 1
- grid_displacements: int32 [12], replicated, may hold values from 0 to 127
- thermostat_heat_level: float32 [12], replicated, may hold values from 0.5 to 2
Outputs:
- final_velocity: float32 [3, 6, 120, 240, 128], P(None, None, 'bx', 'by')
Inputs may be any that keep to these rules, and one draw needn't show every extreme that they name: `bin_population`: A cell's particles fill its first slots. `speed_vectors`: entries in slots at or beyond a cell's occupancy are not read.
All inputs are finite; a program needn't handle non-finite values. No bound on the sum of `approval_flags` on one device may be relied on, other than what follows from the above.
Results may differ from a plain program's by a relative error of at most 0.0003.
Values sent between devices are 32-bit elements; how exact they have to be, the bound alone decides.
No kernel may reach another device: no remote copies, remote signals or barrier semaphores. Data moves between devices by JAX's collectives and lax.ppermute only.
A program may use at most 64 MiB of HBM per device.

v0:
```python
import math
import jax
import jax.numpy as jnp
from jax import lax
from jax.sharding import Mesh
from jax.sharding import PartitionSpec as P

ROUNDS = 6
BX_BY = ("bx_0", "bx_1", "by_0", "by_1", "by_2")
BX = ("bx_0", "bx_1")
BY = ("by_0", "by_1", "by_2")
turn_angle = 130.0 * math.pi / 180.0
drag_gain = 1.0
excess_coupling = 1e-06


def over_axes(array, axes):
    for axis in axes:
        array = lax.psum(array, axis)
    return array


def from_behind(value, axis, steps):
    count = lax.axis_size(axis)
    pairs = [(source, (source + steps) % count) for source in range(count)]
    return lax.ppermute(value, axis, pairs)


def rotate(thermal, spin_choice):
    picked = spin_choice // 2
    unit_axis = [(picked == member).astype(jnp.float32)[None] for member in range(3)]
    sine_term = (math.sin(turn_angle) * (1 - 2 * (spin_choice % 2)).astype(jnp.float32))[None]
    cosine_term = math.cos(turn_angle)
    along_axis = unit_axis[0] * thermal[0] + unit_axis[1] * thermal[1] + unit_axis[2] * thermal[2]
    result = []
    for member in range(3):
        second = (member + 1) % 3
        third_idx = (member + 2) % 3
        cross_term = unit_axis[second] * thermal[third_idx] - unit_axis[third_idx] * thermal[second]
        result.append(
            cosine_term * thermal[member]
            + (1.0 - cosine_term) * unit_axis[member] * along_axis
            + sine_term * cross_term
        )
    return jnp.stack(result)


def per_device(
    speed_vectors,
    bin_population,
    spin_choice,
    approval_flags,
    round_evenness,
    grid_displacements,
    thermostat_heat_level,
):
    slot_count = speed_vectors.shape[1]
    overall_work_sum = over_axes(jnp.sum(bin_population.astype(jnp.float32)), BX_BY)

    def decode(received):
        return (received[1], received[0], received[2])

    def collide_step(
        ensemble_snapshot, bin_tallies, pending, present_round_number, partner_heading
    ):
        slot_rank = lax.broadcasted_iota(jnp.int32, (slot_count,) + bin_tallies.shape, 0)
        occupied = (slot_rank < bin_tallies[None]).astype(jnp.float32)
        moment = jnp.sum(ensemble_snapshot * occupied[None], axis=1)
        cell_mass = bin_tallies.astype(jnp.float32)
        safe_mass = jnp.maximum(cell_mass, 1.0)
        accept_bits = approval_flags[present_round_number].astype(jnp.float32)
        along_moment = moment[partner_heading]
        step_parity = round_evenness[present_round_number]
        stack_parts = (along_moment[None], cell_mass[None], accept_bits[None])
        extent = bin_tallies.shape[partner_heading]
        low_edge = jnp.concatenate(
            [
                lax.slice_in_dim(part_item, 0, 1, axis=partner_heading + 1)
                for part_item in stack_parts
            ],
            0,
        )
        high_edge = jnp.concatenate(
            [
                lax.slice_in_dim(part_item, extent - 1, extent, axis=partner_heading + 1)
                for part_item in stack_parts
            ],
            0,
        )
        if partner_heading == 0:
            start = lax.axis_index(BX) * extent
        else:
            start = lax.axis_index(BY) * extent
        if partner_heading == 0:
            from_above = from_behind(low_edge, BX, -1)
            from_below = from_behind(high_edge, BX, 1)
        else:
            from_above = from_behind(low_edge, BY, -1)
            from_below = from_behind(high_edge, BY, 1)
        above_parts = decode(from_above)
        below_parts = decode(from_below)
        coords = start + lax.broadcasted_iota(jnp.int32, bin_tallies.shape, partner_heading)
        is_lower = (coords - step_parity) % 2 == 0

        def partner(local_values, below_values, above_values):
            extended = jnp.concatenate([below_values, local_values, above_values], partner_heading)
            upper_side = lax.slice_in_dim(extended, 2, extent + 2, axis=partner_heading)
            lower_side = lax.slice_in_dim(extended, 0, extent, axis=partner_heading)
            return jnp.where(is_lower, upper_side, lower_side)

        other_mass = partner(cell_mass, below_parts[0], above_parts[0])
        other_moment = partner(along_moment, below_parts[1], above_parts[1])
        other_bits = partner(accept_bits, below_parts[2], above_parts[2])
        own_speed = pending * along_moment / safe_mass
        other_speed = pending * other_moment / jnp.maximum(other_mass, 1.0)
        closing = jnp.maximum(
            jnp.where(is_lower, own_speed - other_speed, other_speed - own_speed), 0.0
        )
        reduced = cell_mass * other_mass / jnp.maximum(cell_mass + other_mass, 1.0)
        transfer = (
            jnp.maximum(accept_bits, other_bits) * reduced * closing * jnp.tanh(drag_gain * closing)
        )
        new_along = pending * along_moment - jnp.where(is_lower, transfer, -transfer)
        true_moment = jnp.stack(
            [
                new_along if member == partner_heading else pending * moment[member]
                for member in range(3)
            ]
        )
        thermal = (ensemble_snapshot - (moment / safe_mass)[:, None]) * occupied[None]
        kinetic_local = jnp.sum(
            true_moment * true_moment / safe_mass
        ) + pending * pending * jnp.sum(thermal * thermal)
        motion_work_sum = over_axes(kinetic_local, BX_BY)
        speed_multiplier = jnp.sqrt(
            3.0
            * thermostat_heat_level[present_round_number]
            * overall_work_sum
            / (motion_work_sum + excess_coupling)
        )
        turned = rotate(thermal, spin_choice[present_round_number])
        return (
            speed_multiplier
            * ((true_moment / safe_mass)[:, None] * occupied[None] + pending * turned),
            pending,
        )

    def one_round(round_index, carry):
        ensemble_snapshot, bin_tallies, pending = carry
        for displacement_amount in range(2):
            present_round_number = 2 * round_index + displacement_amount
            ensemble_snapshot, pending = collide_step(
                ensemble_snapshot, bin_tallies, pending, present_round_number, displacement_amount
            )
            shift_by = grid_displacements[present_round_number]
            ensemble_snapshot = jnp.roll(ensemble_snapshot, shift_by, axis=4)
            bin_tallies = jnp.roll(bin_tallies, shift_by, axis=2)
        return (ensemble_snapshot, bin_tallies, pending)

    start_scale = jnp.ones((), jnp.float32)
    ensemble_snapshot, bin_tallies, pending = lax.fori_loop(
        0, ROUNDS, one_round, (speed_vectors, bin_population, start_scale)
    )
    return ensemble_snapshot


def solution(mesh):
    split = Mesh(mesh.devices.reshape(4, 2, 2, 4, 2), ("bx_0", "bx_1", "by_0", "by_1", "by_2"))
    return jax.shard_map(
        per_device,
        mesh=split,
        in_specs=(
            P(None, None, BX, BY, None),
            P(BX, BY, None),
            P(None, BX, BY, None),
            P(None, BX, BY, None),
            P(),
            P(),
            P(),
        ),
        out_specs=P(None, None, BX, BY, None),
        check_vma=False,
    )
```

profile of v0, /device:TPU:47, one launch (start us, length us, event | category | flops | bytes accessed | tf_op | source)
XLA Modules:
  0.0 786.4 jit_solution(3658337964983819190)
XLA Ops:
  4.7 7.3 psum.185
  22.4 7.7 psum.188
  30.0 9.8 %psum.189 = f32[]{:T(128)} all-reduce(f32[]{:T(128)} %psum.188), channel_id=1, replica_groups=mesh['bx_0'=4,'bx_1'=2,'by_0'=2,'by_1'=4,'by_2'=2] {'by_2'}, use_global_device_ids=true, to_apply=%region_5.0 | all-reduce | flops 1 | bytes 8 | tf_op jit(solution)/shard_map/psum | solution.py:19
  39.8 746.6 %while.18 = (s32[]{:T(128)}, f32[3,6,15,15,128]{4,3,2,1,0:T(8,128)}, s32[15,15,128]{2,1,0:T(8,128)S(1)}, f32[12]{0:T(128)}, f32[]{:T(128)}, /*index=5*/s32[12]{0...) while((s32[]{:T(128)}, ...), condition=%wide.region_23.26_spmd, body=%wide.region_6.25_spmd.sunk | while | flops 29883296 | bytes 69046136 | solution.py:161
  70.2 8.8 %psum.200 = f32[]{:T(128)} all-reduce(f32[]{:T(128)S(6)} %add.745), channel_id=1, replica_groups=mesh['bx_0'=4,'bx_1'=2,'by_0'=2,'by_1'=4,'by_2'=2] {'bx_0'}, use_global_device_ids=true, to_apply=%region_10.10 | all-reduce | flops 1 | bytes 8 | tf_op jit(solution)/shard_map/while/body/eval_jaxpr/psum | solution.py:19
  79.0 6.0 psum.201
  90.6 9.1 %psum.203 = f32[]{:T(128)} all-reduce(f32[]{:T(128)} %psum.202), channel_id=1, replica_groups=mesh['bx_0'=4,'bx_1'=2,'by_0'=2,'by_1'=4,'by_2'=2] {'by_1'}, use_global_device_ids=true, to_apply=%region_13.13 | all-reduce | flops 1 | bytes 8 | tf_op jit(solution)/shard_map/while/body/eval_jaxpr/psum | solution.py:19
  100.4 9.9 %psum.204 = f32[]{:T(128)} all-reduce(f32[]{:T(128)} %psum.203), channel_id=1, replica_groups=mesh['bx_0'=4,'bx_1'=2,'by_0'=2,'by_1'=4,'by_2'=2] {'by_2'}, use_global_device_ids=true, to_apply=%region_14.14 | all-reduce | flops 1 | bytes 8 | tf_op jit(solution)/shard_map/while/body/eval_jaxpr/psum | solution.py:19
  122.5 7.2 psum.205
  129.7 5.9 psum.206
  141.2 7.4 psum.208
  148.6 12.5 %psum.209 = f32[]{:T(128)} all-reduce(f32[]{:T(128)} %psum.208), channel_id=1, replica_groups=mesh['bx_0'=4,'bx_1'=2,'by_0'=2,'by_1'=4,'by_2'=2] {'by_2'}, use_global_device_ids=true, to_apply=%region_22.24 | all-reduce | flops 1 | bytes 8 | tf_op jit(solution)/shard_map/while/body/eval_jaxpr/psum | solution.py:19
  196.9 7.3 psum.200
  204.3 6.0 psum.201
  216.0 6.3 psum.203
  222.9 9.9 %psum.204 = f32[]{:T(128)} all-reduce(f32[]{:T(128)} %psum.203), channel_id=1, replica_groups=mesh['bx_0'=4,'bx_1'=2,'by_0'=2,'by_1'=4,'by_2'=2] {'by_2'}, use_global_device_ids=true, to_apply=%region_14.14 | all-reduce | flops 1 | bytes 8 | tf_op jit(solution)/shard_map/while/body/eval_jaxpr/psum | solution.py:19
  245.0 8.4 %psum.205 = f32[]{:T(128)} all-reduce(f32[]{:T(128)S(6)} %add.749), channel_id=1, replica_groups=mesh['bx_0'=4,'bx_1'=2,'by_0'=2,'by_1'=4,'by_2'=2] {'bx_0'}, use_global_device_ids=true, to_apply=%region_18.20 | all-reduce | flops 1 | bytes 8 | tf_op jit(solution)/shard_map/while/body/eval_jaxpr/psum | solution.py:19
  253.4 5.9 psum.206
  264.9 8.5 %psum.208 = f32[]{:T(128)} all-reduce(f32[]{:T(128)} %psum.207), channel_id=1, replica_groups=mesh['bx_0'=4,'bx_1'=2,'by_0'=2,'by_1'=4,'by_2'=2] {'by_1'}, use_global_device_ids=true, to_apply=%region_21.23 | all-reduce | flops 1 | bytes 8 | tf_op jit(solution)/shard_map/while/body/eval_jaxpr/psum | solution.py:19
  273.4 11.7 %psum.209 = f32[]{:T(128)} all-reduce(f32[]{:T(128)} %psum.208), channel_id=1, replica_groups=mesh['bx_0'=4,'bx_1'=2,'by_0'=2,'by_1'=4,'by_2'=2] {'by_2'}, use_global_device_ids=true, to_apply=%region_22.24 | all-reduce | flops 1 | bytes 8 | tf_op jit(solution)/shard_map/while/body/eval_jaxpr/psum | solution.py:19
  321.1 6.6 psum.200
  327.7 6.0 psum.201
  339.4 6.3 psum.203
  346.3 9.6 %psum.204 = f32[]{:T(128)} all-reduce(f32[]{:T(128)} %psum.203), channel_id=1, replica_groups=mesh['bx_0'=4,'bx_1'=2,'by_0'=2,'by_1'=4,'by_2'=2] {'by_2'}, use_global_device_ids=true, to_apply=%region_14.14 | all-reduce | flops 1 | bytes 8 | tf_op jit(solution)/shard_map/while/body/eval_jaxpr/psum | solution.py:19
  368.0 9.4 %psum.205 = f32[]{:T(128)} all-reduce(f32[]{:T(128)S(6)} %add.749), channel_id=1, replica_groups=mesh['bx_0'=4,'bx_1'=2,'by_0'=2,'by_1'=4,'by_2'=2] {'bx_0'}, use_global_device_ids=true, to_apply=%region_18.20 | all-reduce | flops 1 | bytes 8 | tf_op jit(solution)/shard_map/while/body/eval_jaxpr/psum | solution.py:19
  389.0 8.5 %psum.208 = f32[]{:T(128)} all-reduce(f32[]{:T(128)} %psum.207), channel_id=1, replica_groups=mesh['bx_0'=4,'bx_1'=2,'by_0'=2,'by_1'=4,'by_2'=2] {'by_1'}, use_global_device_ids=true, to_apply=%region_21.23 | all-reduce | flops 1 | bytes 8 | tf_op jit(solution)/shard_map/while/body/eval_jaxpr/psum | solution.py:19
  397.5 11.3 %psum.209 = f32[]{:T(128)} all-reduce(f32[]{:T(128)} %psum.208), channel_id=1, replica_groups=mesh['bx_0'=4,'bx_1'=2,'by_0'=2,'by_1'=4,'by_2'=2] {'by_2'}, use_global_device_ids=true, to_apply=%region_22.24 | all-reduce | flops 1 | bytes 8 | tf_op jit(solution)/shard_map/while/body/eval_jaxpr/psum | solution.py:19
  444.8 6.6 psum.200
  451.4 6.0 psum.201
  463.1 6.3 psum.203
  470.0 9.6 %psum.204 = f32[]{:T(128)} all-reduce(f32[]{:T(128)} %psum.203), channel_id=1, replica_groups=mesh['bx_0'=4,'bx_1'=2,'by_0'=2,'by_1'=4,'by_2'=2] {'by_2'}, use_global_device_ids=true, to_apply=%region_14.14 | all-reduce | flops 1 | bytes 8 | tf_op jit(solution)/shard_map/while/body/eval_jaxpr/psum | solution.py:19
  491.8 9.4 %psum.205 = f32[]{:T(128)} all-reduce(f32[]{:T(128)S(6)} %add.749), channel_id=1, replica_groups=mesh['bx_0'=4,'bx_1'=2,'by_0'=2,'by_1'=4,'by_2'=2] {'bx_0'}, use_global_device_ids=true, to_apply=%region_18.20 | all-reduce | flops 1 | bytes 8 | tf_op jit(solution)/shard_map/while/body/eval_jaxpr/psum | solution.py:19
  512.8 8.5 %psum.208 = f32[]{:T(128)} all-reduce(f32[]{:T(128)} %psum.207), channel_id=1, replica_groups=mesh['bx_0'=4,'bx_1'=2,'by_0'=2,'by_1'=4,'by_2'=2] {'by_1'}, use_global_device_ids=true, to_apply=%region_21.23 | all-reduce | flops 1 | bytes 8 | tf_op jit(solution)/shard_map/while/body/eval_jaxpr/psum | solution.py:19
  521.3 11.7 %psum.209 = f32[]{:T(128)} all-reduce(f32[]{:T(128)} %psum.208), channel_id=1, replica_groups=mesh['bx_0'=4,'bx_1'=2,'by_0'=2,'by_1'=4,'by_2'=2] {'by_2'}, use_global_device_ids=true, to_apply=%region_22.24 | all-reduce | flops 1 | bytes 8 | tf_op jit(solution)/shard_map/while/body/eval_jaxpr/psum | solution.py:19
  568.9 6.6 psum.200
  575.5 6.0 psum.201
  587.2 6.3 psum.203
  594.1 9.6 %psum.204 = f32[]{:T(128)} all-reduce(f32[]{:T(128)} %psum.203), channel_id=1, replica_groups=mesh['bx_0'=4,'bx_1'=2,'by_0'=2,'by_1'=4,'by_2'=2] {'by_2'}, use_global_device_ids=true, to_apply=%region_14.14 | all-reduce | flops 1 | bytes 8 | tf_op jit(solution)/shard_map/while/body/eval_jaxpr/psum | solution.py:19
  615.9 9.4 %psum.205 = f32[]{:T(128)} all-reduce(f32[]{:T(128)S(6)} %add.749), channel_id=1, replica_groups=mesh['bx_0'=4,'bx_1'=2,'by_0'=2,'by_1'=4,'by_2'=2] {'bx_0'}, use_global_device_ids=true, to_apply=%region_18.20 | all-reduce | flops 1 | bytes 8 | tf_op jit(solution)/shard_map/while/body/eval_jaxpr/psum | solution.py:19
  636.9 8.5 %psum.208 = f32[]{:T(128)} all-reduce(f32[]{:T(128)} %psum.207), channel_id=1, replica_groups=mesh['bx_0'=4,'bx_1'=2,'by_0'=2,'by_1'=4,'by_2'=2] {'by_1'}, use_global_device_ids=true, to_apply=%region_21.23 | all-reduce | flops 1 | bytes 8 | tf_op jit(solution)/shard_map/while/body/eval_jaxpr/psum | solution.py:19
  645.4 11.3 %psum.209 = f32[]{:T(128)} all-reduce(f32[]{:T(128)} %psum.208), channel_id=1, replica_groups=mesh['bx_0'=4,'bx_1'=2,'by_0'=2,'by_1'=4,'by_2'=2] {'by_2'}, use_global_device_ids=true, to_apply=%region_22.24 | all-reduce | flops 1 | bytes 8 | tf_op jit(solution)/shard_map/while/body/eval_jaxpr/psum | solution.py:19
  692.6 6.6 psum.200
  699.3 6.0 psum.201
  710.9 6.3 psum.203
  717.9 9.6 %psum.204 = f32[]{:T(128)} all-reduce(f32[]{:T(128)} %psum.203), channel_id=1, replica_groups=mesh['bx_0'=4,'bx_1'=2,'by_0'=2,'by_1'=4,'by_2'=2] {'by_2'}, use_global_device_ids=true, to_apply=%region_14.14 | all-reduce | flops 1 | bytes 8 | tf_op jit(solution)/shard_map/while/body/eval_jaxpr/psum | solution.py:19
  739.6 9.4 %psum.205 = f32[]{:T(128)} all-reduce(f32[]{:T(128)S(6)} %add.749), channel_id=1, replica_groups=mesh['bx_0'=4,'bx_1'=2,'by_0'=2,'by_1'=4,'by_2'=2] {'bx_0'}, use_global_device_ids=true, to_apply=%region_18.20 | all-reduce | flops 1 | bytes 8 | tf_op jit(solution)/shard_map/while/body/eval_jaxpr/psum | solution.py:19
  760.6 8.5 %psum.208 = f32[]{:T(128)} all-reduce(f32[]{:T(128)} %psum.207), channel_id=1, replica_groups=mesh['bx_0'=4,'bx_1'=2,'by_0'=2,'by_1'=4,'by_2'=2] {'by_1'}, use_global_device_ids=true, to_apply=%region_21.23 | all-reduce | flops 1 | bytes 8 | tf_op jit(solution)/shard_map/while/body/eval_jaxpr/psum | solution.py:19
  769.1 11.7 %psum.209 = f32[]{:T(128)} all-reduce(f32[]{:T(128)} %psum.208), channel_id=1, replica_groups=mesh['bx_0'=4,'bx_1'=2,'by_0'=2,'by_1'=4,'by_2'=2] {'by_2'}, use_global_device_ids=true, to_apply=%region_22.24 | all-reduce | flops 1 | bytes 8 | tf_op jit(solution)/shard_map/while/body/eval_jaxpr/psum | solution.py:19
  (481 shorter events, 334.0 us)
Async XLA Ops:
  0.9 38.9 %copy-start.8 = (s32[12]{0:T(128)S(1)}, s32[12]{0:T(128)}, u32[]{:S(2)}) copy-start(s32[12]{0:T(128)} %param.17) | copy-start | bytes 148
  0.9 38.9 %copy-start.10 = (s32[12]{0:T(128)S(1)}, s32[12]{0:T(128)}, u32[]{:S(2)}) copy-start(s32[12]{0:T(128)} %param.18) | copy-start | bytes 148
  46.4 14.8 %collective-permute-start.1 = (f32[3,1,15,128]{3,2,1,0:T(8,128)}, f32[3,1,15,128]{3,2,1,0:T(8,128)}, u32[]{:S(2)}, u32[]{:S(2)}) collective-permute-start(f32[3,1,15,128]{3,2,1,0:T(8,128)} %pad_maximum_fusion.23), channel_id=1, source_target_pairs={{0,112},{16,0},{32,16},{48,32},{64,48},{80,64},{96,80},{112,96},{1... | collective-permute-start | bytes 69128 | tf_op jit(solution)/shard_map/while/body/eval_jaxpr/ppermute | solution.py:26
  48.1 14.0 %collective-permute-start = (f32[3,1,15,128]{3,2,1,0:T(8,128)}, f32[3,1,15,128]{3,2,1,0:T(8,128)}, u32[]{:S(2)}, u32[]{:S(2)}) collective-permute-start(f32[3,1,15,128]{3,2,1,0:T(8,128)} %pad_maximum_fusion.22), channel_id=1, source_target_pairs={{0,16},{16,32},{32,48},{48,64},{64,80},{80,96},{96,112},{112,0},{1... | collective-permute-start | bytes 69128 | tf_op jit(solution)/shard_map/while/body/eval_jaxpr/ppermute | solution.py:26
  65.7 19.2 %copy-start.7 = (f32[12]{0:T(128)S(1)}, f32[12]{0:T(128)}, u32[]{:S(2)}) copy-start(f32[12]{0:T(128)} %get-tuple-element.660) | copy-start | bytes 148 | tf_op jit(solution)/shard_map/while
  65.7 45.4 %copy-start.1 = (f32[15,15,128]{2,1,0:T(8,128)S(1)}, f32[15,15,128]{2,1,0:T(8,128)}, u32[]{:S(2)}) copy-start(f32[15,15,128]{2,1,0:T(8,128)} %get-tuple-element.553) | copy-start | bytes 345604 | tf_op jit(solution)/shard_map/while
  65.7 45.4 %copy-start.2 = (f32[15,15,128]{2,1,0:T(8,128)S(1)}, f32[15,15,128]{2,1,0:T(8,128)}, u32[]{:S(2)}) copy-start(f32[15,15,128]{2,1,0:T(8,128)} %get-tuple-element.561) | copy-start | bytes 345604 | tf_op jit(solution)/shard_map/while
  65.7 45.4 %copy-start.3 = (f32[15,15,128]{2,1,0:T(8,128)S(1)}, f32[15,15,128]{2,1,0:T(8,128)}, u32[]{:S(2)}) copy-start(f32[15,15,128]{2,1,0:T(8,128)} %get-tuple-element.556) | copy-start | bytes 345604 | tf_op jit(solution)/shard_map/while
  115.1 3.4 collective-permute-start.3
  115.5 2.9 collective-permute-start.2
  173.1 14.8 %collective-permute-start.1 = (f32[3,1,15,128]{3,2,1,0:T(8,128)}, f32[3,1,15,128]{3,2,1,0:T(8,128)}, u32[]{:S(2)}, u32[]{:S(2)}) collective-permute-start(f32[3,1,15,128]{3,2,1,0:T(8,128)} %pad_maximum_fusion.23), channel_id=1, source_target_pairs={{0,112},{16,0},{32,16},{48,32},{64,48},{80,64},{96,80},{112,96},{1... | collective-permute-start | bytes 69128 | tf_op jit(solution)/shard_map/while/body/eval_jaxpr/ppermute | solution.py:26
  174.1 14.8 %collective-permute-start = (f32[3,1,15,128]{3,2,1,0:T(8,128)}, f32[3,1,15,128]{3,2,1,0:T(8,128)}, u32[]{:S(2)}, u32[]{:S(2)}) collective-permute-start(f32[3,1,15,128]{3,2,1,0:T(8,128)} %pad_maximum_fusion.22), channel_id=1, source_target_pairs={{0,16},{16,32},{32,48},{48,64},{64,80},{80,96},{96,112},{112,0},{1... | collective-permute-start | bytes 69128 | tf_op jit(solution)/shard_map/while/body/eval_jaxpr/ppermute | solution.py:26
  192.5 17.8 %copy-start.7 = (f32[12]{0:T(128)S(1)}, f32[12]{0:T(128)}, u32[]{:S(2)}) copy-start(f32[12]{0:T(128)} %get-tuple-element.660) | copy-start | bytes 148 | tf_op jit(solution)/shard_map/while
  192.5 41.2 %copy-start.1 = (f32[15,15,128]{2,1,0:T(8,128)S(1)}, f32[15,15,128]{2,1,0:T(8,128)}, u32[]{:S(2)}) copy-start(f32[15,15,128]{2,1,0:T(8,128)} %get-tuple-element.553) | copy-start | bytes 345604 | tf_op jit(solution)/shard_map/while
  192.5 41.2 %copy-start.2 = (f32[15,15,128]{2,1,0:T(8,128)S(1)}, f32[15,15,128]{2,1,0:T(8,128)}, u32[]{:S(2)}) copy-start(f32[15,15,128]{2,1,0:T(8,128)} %get-tuple-element.561) | copy-start | bytes 345604 | tf_op jit(solution)/shard_map/while
  192.5 41.2 %copy-start.3 = (f32[15,15,128]{2,1,0:T(8,128)S(1)}, f32[15,15,128]{2,1,0:T(8,128)}, u32[]{:S(2)}) copy-start(f32[15,15,128]{2,1,0:T(8,128)} %get-tuple-element.556) | copy-start | bytes 345604 | tf_op jit(solution)/shard_map/while
  237.6 3.3 collective-permute-start.3
  238.0 2.9 collective-permute-start.2
  297.3 14.8 %collective-permute-start.1 = (f32[3,1,15,128]{3,2,1,0:T(8,128)}, f32[3,1,15,128]{3,2,1,0:T(8,128)}, u32[]{:S(2)}, u32[]{:S(2)}) collective-permute-start(f32[3,1,15,128]{3,2,1,0:T(8,128)} %pad_maximum_fusion.23), channel_id=1, source_target_pairs={{0,112},{16,0},{32,16},{48,32},{64,48},{80,64},{96,80},{112,96},{1... | collective-permute-start | bytes 69128 | tf_op jit(solution)/shard_map/while/body/eval_jaxpr/ppermute | solution.py:26
  298.2 14.8 %collective-permute-start = (f32[3,1,15,128]{3,2,1,0:T(8,128)}, f32[3,1,15,128]{3,2,1,0:T(8,128)}, u32[]{:S(2)}, u32[]{:S(2)}) collective-permute-start(f32[3,1,15,128]{3,2,1,0:T(8,128)} %pad_maximum_fusion.22), channel_id=1, source_target_pairs={{0,16},{16,32},{32,48},{48,64},{64,80},{80,96},{96,112},{112,0},{1... | collective-permute-start | bytes 69128 | tf_op jit(solution)/shard_map/while/body/eval_jaxpr/ppermute | solution.py:26
  316.6 17.1 %copy-start.7 = (f32[12]{0:T(128)S(1)}, f32[12]{0:T(128)}, u32[]{:S(2)}) copy-start(f32[12]{0:T(128)} %get-tuple-element.660) | copy-start | bytes 148 | tf_op jit(solution)/shard_map/while
  316.6 40.1 %copy-start.1 = (f32[15,15,128]{2,1,0:T(8,128)S(1)}, f32[15,15,128]{2,1,0:T(8,128)}, u32[]{:S(2)}) copy-start(f32[15,15,128]{2,1,0:T(8,128)} %get-tuple-element.553) | copy-start | bytes 345604 | tf_op jit(solution)/shard_map/while
  316.6 40.1 %copy-start.2 = (f32[15,15,128]{2,1,0:T(8,128)S(1)}, f32[15,15,128]{2,1,0:T(8,128)}, u32[]{:S(2)}) copy-start(f32[15,15,128]{2,1,0:T(8,128)} %get-tuple-element.561) | copy-start | bytes 345604 | tf_op jit(solution)/shard_map/while
  316.6 40.1 %copy-start.3 = (f32[15,15,128]{2,1,0:T(8,128)S(1)}, f32[15,15,128]{2,1,0:T(8,128)}, u32[]{:S(2)}) copy-start(f32[15,15,128]{2,1,0:T(8,128)} %get-tuple-element.556) | copy-start | bytes 345604 | tf_op jit(solution)/shard_map/while
  360.7 3.3 collective-permute-start.3
  361.1 2.9 collective-permute-start.2
  421.0 14.8 %collective-permute-start.1 = (f32[3,1,15,128]{3,2,1,0:T(8,128)}, f32[3,1,15,128]{3,2,1,0:T(8,128)}, u32[]{:S(2)}, u32[]{:S(2)}) collective-permute-start(f32[3,1,15,128]{3,2,1,0:T(8,128)} %pad_maximum_fusion.23), channel_id=1, source_target_pairs={{0,112},{16,0},{32,16},{48,32},{64,48},{80,64},{96,80},{112,96},{1... | collective-permute-start | bytes 69128 | tf_op jit(solution)/shard_map/while/body/eval_jaxpr/ppermute | solution.py:26
  421.9 14.8 %collective-permute-start = (f32[3,1,15,128]{3,2,1,0:T(8,128)}, f32[3,1,15,128]{3,2,1,0:T(8,128)}, u32[]{:S(2)}, u32[]{:S(2)}) collective-permute-start(f32[3,1,15,128]{3,2,1,0:T(8,128)} %pad_maximum_fusion.22), channel_id=1, source_target_pairs={{0,16},{16,32},{32,48},{48,64},{64,80},{80,96},{96,112},{112,0},{1... | collective-permute-start | bytes 69128 | tf_op jit(solution)/shard_map/while/body/eval_jaxpr/ppermute | solution.py:26
  440.3 40.1 %copy-start.1 = (f32[15,15,128]{2,1,0:T(8,128)S(1)}, f32[15,15,128]{2,1,0:T(8,128)}, u32[]{:S(2)}) copy-start(f32[15,15,128]{2,1,0:T(8,128)} %get-tuple-element.553) | copy-start | bytes 345604 | tf_op jit(solution)/shard_map/while
  440.3 40.1 %copy-start.2 = (f32[15,15,128]{2,1,0:T(8,128)S(1)}, f32[15,15,128]{2,1,0:T(8,128)}, u32[]{:S(2)}) copy-start(f32[15,15,128]{2,1,0:T(8,128)} %get-tuple-element.561) | copy-start | bytes 345604 | tf_op jit(solution)/shard_map/while
  440.3 40.1 %copy-start.3 = (f32[15,15,128]{2,1,0:T(8,128)S(1)}, f32[15,15,128]{2,1,0:T(8,128)}, u32[]{:S(2)}) copy-start(f32[15,15,128]{2,1,0:T(8,128)} %get-tuple-element.556) | copy-start | bytes 345604 | tf_op jit(solution)/shard_map/while
  484.4 3.3 collective-permute-start.3
  484.8 2.9 collective-permute-start.2
  545.1 14.8 %collective-permute-start.1 = (f32[3,1,15,128]{3,2,1,0:T(8,128)}, f32[3,1,15,128]{3,2,1,0:T(8,128)}, u32[]{:S(2)}, u32[]{:S(2)}) collective-permute-start(f32[3,1,15,128]{3,2,1,0:T(8,128)} %pad_maximum_fusion.23), channel_id=1, source_target_pairs={{0,112},{16,0},{32,16},{48,32},{64,48},{80,64},{96,80},{112,96},{1... | collective-permute-start | bytes 69128 | tf_op jit(solution)/shard_map/while/body/eval_jaxpr/ppermute | solution.py:26
  546.0 14.8 %collective-permute-start = (f32[3,1,15,128]{3,2,1,0:T(8,128)}, f32[3,1,15,128]{3,2,1,0:T(8,128)}, u32[]{:S(2)}, u32[]{:S(2)}) collective-permute-start(f32[3,1,15,128]{3,2,1,0:T(8,128)} %pad_maximum_fusion.22), channel_id=1, source_target_pairs={{0,16},{16,32},{32,48},{48,64},{64,80},{80,96},{96,112},{112,0},{1... | collective-permute-start | bytes 69128 | tf_op jit(solution)/shard_map/while/body/eval_jaxpr/ppermute | solution.py:26
  564.4 17.1 %copy-start.7 = (f32[12]{0:T(128)S(1)}, f32[12]{0:T(128)}, u32[]{:S(2)}) copy-start(f32[12]{0:T(128)} %get-tuple-element.660) | copy-start | bytes 148 | tf_op jit(solution)/shard_map/while
  564.4 40.1 %copy-start.1 = (f32[15,15,128]{2,1,0:T(8,128)S(1)}, f32[15,15,128]{2,1,0:T(8,128)}, u32[]{:S(2)}) copy-start(f32[15,15,128]{2,1,0:T(8,128)} %get-tuple-element.553) | copy-start | bytes 345604 | tf_op jit(solution)/shard_map/while
  564.4 40.1 %copy-start.2 = (f32[15,15,128]{2,1,0:T(8,128)S(1)}, f32[15,15,128]{2,1,0:T(8,128)}, u32[]{:S(2)}) copy-start(f32[15,15,128]{2,1,0:T(8,128)} %get-tuple-element.561) | copy-start | bytes 345604 | tf_op jit(solution)/shard_map/while
  564.4 40.1 %copy-start.3 = (f32[15,15,128]{2,1,0:T(8,128)S(1)}, f32[15,15,128]{2,1,0:T(8,128)}, u32[]{:S(2)}) copy-start(f32[15,15,128]{2,1,0:T(8,128)} %get-tuple-element.556) | copy-start | bytes 345604 | tf_op jit(solution)/shard_map/while
  608.5 3.3 collective-permute-start.3
  609.0 2.9 collective-permute-start.2
  668.8 14.8 %collective-permute-start.1 = (f32[3,1,15,128]{3,2,1,0:T(8,128)}, f32[3,1,15,128]{3,2,1,0:T(8,128)}, u32[]{:S(2)}, u32[]{:S(2)}) collective-permute-start(f32[3,1,15,128]{3,2,1,0:T(8,128)} %pad_maximum_fusion.23), channel_id=1, source_target_pairs={{0,112},{16,0},{32,16},{48,32},{64,48},{80,64},{96,80},{112,96},{1... | collective-permute-start | bytes 69128 | tf_op jit(solution)/shard_map/while/body/eval_jaxpr/ppermute | solution.py:26
  669.8 14.8 %collective-permute-start = (f32[3,1,15,128]{3,2,1,0:T(8,128)}, f32[3,1,15,128]{3,2,1,0:T(8,128)}, u32[]{:S(2)}, u32[]{:S(2)}) collective-permute-start(f32[3,1,15,128]{3,2,1,0:T(8,128)} %pad_maximum_fusion.22), channel_id=1, source_target_pairs={{0,16},{16,32},{32,48},{48,64},{64,80},{80,96},{96,112},{112,0},{1... | collective-permute-start | bytes 69128 | tf_op jit(solution)/shard_map/while/body/eval_jaxpr/ppermute | solution.py:26
  688.2 40.1 %copy-start.1 = (f32[15,15,128]{2,1,0:T(8,128)S(1)}, f32[15,15,128]{2,1,0:T(8,128)}, u32[]{:S(2)}) copy-start(f32[15,15,128]{2,1,0:T(8,128)} %get-tuple-element.553) | copy-start | bytes 345604 | tf_op jit(solution)/shard_map/while
  688.2 40.1 %copy-start.2 = (f32[15,15,128]{2,1,0:T(8,128)S(1)}, f32[15,15,128]{2,1,0:T(8,128)}, u32[]{:S(2)}) copy-start(f32[15,15,128]{2,1,0:T(8,128)} %get-tuple-element.561) | copy-start | bytes 345604 | tf_op jit(solution)/shard_map/while
  688.2 40.1 %copy-start.3 = (f32[15,15,128]{2,1,0:T(8,128)S(1)}, f32[15,15,128]{2,1,0:T(8,128)}, u32[]{:S(2)}) copy-start(f32[15,15,128]{2,1,0:T(8,128)} %get-tuple-element.556) | copy-start | bytes 345604 | tf_op jit(solution)/shard_map/while
  732.2 3.3 collective-permute-start.3
  732.7 2.9 collective-permute-start.2
  (38 other events, 164.5 us)
where the time goes:
time: 790 us; the launch traced here: 786 us
  blocking collectives  474 us (60%)
  other arithmetic  171 us (22%)
  loops' own time  65 us (8%)
  starting transfers between devices  34.5 us (4%)
  local copies, waits for them, and re-layouts  33.5 us (4%)
  waiting for transfers between devices  8.47 us (1%)
    psum x65, blocking collectives, over_axes(): array = lax.psum(array, axis)  474 us
    another operation x1, loops' own time, per_device(): lax.fori_loop(0, ROUNDS, one_round, (speed_vectors, bin_population, start...  65 us
    ppermute x24, starting transfers between devices, from_behind(): return lax.ppermute(value, axis, pairs)  34.5 us
    reduce_sum x12, other arithmetic, collide_step(): jnp.sum(thermal * thermal)  26.1 us
    add x12, other arithmetic, rotate(): cosine_term * thermal[member]  25.3 us
    reduce_sum x12, other arithmetic, collide_step(): moment = jnp.sum(ensemble_snapshot * occupied[None], axis=1)  18.5 us
  transfers between devices with their start and end apart: 24, of which 6 were waited for; matrix products, arithmetic and copies ran while one was open for 8% of the time, Pallas kernels for 0%

commit v1 on v0

--- a/solution.py
+++ b/solution.py
@@ -16,7 +16,7 @@
 
 def over_axes(array, axes):
     for axis in axes:
-        array = lax.psum(array, axis)
+        array = jnp.sum(lax.all_gather(array, axis), axis=0)
     return array
 
 

time: 790 us -> 939 us (1.19)
  local copies, waits for them, and re-layouts: 33.5 us -> 163 us
  other arithmetic: 171 us -> 226 us
  blocking collectives: 474 us -> 435 us
    psum x65 -> x0, blocking collectives: 474 us -> none  [over_axes(): array = lax.psum(array, axis)]
    while x0 -> x60, blocking collectives: none -> 403 us
    while x120 -> x378, local copies, waits for them, and re-layouts: 0.29 us -> 116 us
    reduce_sum x0 -> x65, other arithmetic: none -> 41.9 us  [over_axes(): array = jnp.sum(lax.all_gather(array, axis), axis=0)]
    unnamed x0 -> x5, blocking collectives: none -> 31.8 us
    unnamed x6 -> x31, local copies, waits for them, and re-layouts: 4.07 us -> 13.8 us
  transfers between devices with their start and end apart: 24 -> 24, of which waited for: 6 -> 6; matrix products, arithmetic and copies ran while one was open for 8% -> 11% of each run, Pallas kernels for 0% -> 0%
where the time goes in v1:
time: 939 us; the launch traced here: 934 us
  blocking collectives  435 us (46%)
  other arithmetic  226 us (24%)
  local copies, waits for them, and re-layouts  163 us (17%)
  loops' own time  67.8 us (7%)
  starting transfers between devices  34.5 us (4%)
    while x60, blocking collectives  403 us
    while x378, local copies, waits for them, and re-layouts  116 us
    another operation x1, loops' own time, per_device(): lax.fori_loop(0, ROUNDS, one_round, (speed_vectors, bin_population, start...  67.8 us
    reduce_sum x65, other arithmetic, over_axes(): array = jnp.sum(lax.all_gather(array, axis), axis=0)  41.9 us
    ppermute x24, starting transfers between devices, from_behind(): return lax.ppermute(value, axis, pairs)  34.5 us
    unnamed x5, blocking collectives  31.8 us
    reduce_sum x12, other arithmetic, collide_step(): jnp.sum(thermal * thermal)  26.4 us
    add x12, other arithmetic, rotate(): cosine_term * thermal[member]  25.3 us
  transfers between devices with their start and end apart: 24, of which 6 were waited for; matrix products, arithmetic and copies ran while one was open for 11% of the time, Pallas kernels for 0%

profile of v1, /device:TPU:47, one launch (start us, length us, event | category | flops | bytes accessed | tf_op | source)
XLA Modules:
  0.0 933.9 jit_solution(9526465459926051743)
XLA Ops:
  6.8 6.7 all-reduce.10
  16.1 5.3 all-reduce.11
  30.3 7.0 all-reduce.13
  40.0 9.1 all-reduce.14
  49.7 884.2 %while.18 = (s32[]{:T(128)}, f32[3,6,15,15,128]{4,3,2,1,0:T(8,128)}, s32[15,15,128]{2,1,0:T(8,128)S(1)}, f32[12]{0:T(128)}, f32[]{:T(128)}, /*index=5*/s32[12]{0...) while((s32[]{:T(128)}, ...), condition=%wide.region_23.26_spmd, body=%wide.region_6.25_spmd.sunk | while | flops 29883344 | bytes 69058264 | solution.py:161
  88.3 8.2 all-reduce.25
  115.0 8.5 all-reduce.28
  126.4 9.4 %all-reduce.29 = f32[2]{0:T(128)S(1)} all-reduce(f32[2]{0:T(128)S(1)} %dynamic-update-slice.29), channel_id=1, replica_groups=mesh['bx_0'=4,'bx_1'=2,'by_0'=2,'by_1'=4,'by_2'=2] {'by_2'}, use_global_device_ids=true, to_apply=%add.4 | all-reduce | flops 2 | bytes 16 | tf_op jit(solution)/shard_map/while
  149.6 6.6 all-reduce.30
  158.2 5.3 all-reduce.31
  172.4 6.8 all-reduce.33
  181.3 11.8 %all-reduce.34 = f32[2]{0:T(128)S(1)} all-reduce(f32[2]{0:T(128)S(1)} %dynamic-update-slice.34), channel_id=1, replica_groups=mesh['bx_0'=4,'bx_1'=2,'by_0'=2,'by_1'=4,'by_2'=2] {'by_2'}, use_global_device_ids=true, to_apply=%add.9 | all-reduce | flops 2 | bytes 16 | tf_op jit(solution)/shard_map/while
  238.0 6.7 all-reduce.25
  263.3 5.7 all-reduce.28
  271.9 9.4 %all-reduce.29 = f32[2]{0:T(128)S(1)} all-reduce(f32[2]{0:T(128)S(1)} %dynamic-update-slice.29), channel_id=1, replica_groups=mesh['bx_0'=4,'bx_1'=2,'by_0'=2,'by_1'=4,'by_2'=2] {'by_2'}, use_global_device_ids=true, to_apply=%add.4 | all-reduce | flops 2 | bytes 16 | tf_op jit(solution)/shard_map/while
  295.0 7.8 all-reduce.30
  304.9 5.3 all-reduce.31
  319.0 7.7 all-reduce.33
  328.8 11.4 %all-reduce.34 = f32[2]{0:T(128)S(1)} all-reduce(f32[2]{0:T(128)S(1)} %dynamic-update-slice.34), channel_id=1, replica_groups=mesh['bx_0'=4,'bx_1'=2,'by_0'=2,'by_1'=4,'by_2'=2] {'by_2'}, use_global_device_ids=true, to_apply=%add.9 | all-reduce | flops 2 | bytes 16 | tf_op jit(solution)/shard_map/while
  385.1 6.0 all-reduce.25
  409.7 5.7 all-reduce.28
  418.2 9.0 all-reduce.29
  441.0 8.9 all-reduce.30
  451.9 5.3 all-reduce.31
  466.1 7.7 all-reduce.33
  475.9 11.0 %all-reduce.34 = f32[2]{0:T(128)S(1)} all-reduce(f32[2]{0:T(128)S(1)} %dynamic-update-slice.34), channel_id=1, replica_groups=mesh['bx_0'=4,'bx_1'=2,'by_0'=2,'by_1'=4,'by_2'=2] {'by_2'}, use_global_device_ids=true, to_apply=%add.9 | all-reduce | flops 2 | bytes 16 | tf_op jit(solution)/shard_map/while
  531.7 6.0 all-reduce.25
  541.1 5.3 all-reduce.26
  556.3 5.7 all-reduce.28
  564.9 9.0 all-reduce.29
  587.7 8.9 all-reduce.30
  598.6 5.3 all-reduce.31
  612.8 7.7 all-reduce.33
  622.5 11.4 %all-reduce.34 = f32[2]{0:T(128)S(1)} all-reduce(f32[2]{0:T(128)S(1)} %dynamic-update-slice.34), channel_id=1, replica_groups=mesh['bx_0'=4,'bx_1'=2,'by_0'=2,'by_1'=4,'by_2'=2] {'by_2'}, use_global_device_ids=true, to_apply=%add.9 | all-reduce | flops 2 | bytes 16 | tf_op jit(solution)/shard_map/while
  678.8 6.0 all-reduce.25
  703.4 5.7 all-reduce.28
  711.9 9.0 all-reduce.29
  734.8 8.9 all-reduce.30
  745.6 5.3 all-reduce.31
  759.8 7.7 all-reduce.33
  769.6 11.0 %all-reduce.34 = f32[2]{0:T(128)S(1)} all-reduce(f32[2]{0:T(128)S(1)} %dynamic-update-slice.34), channel_id=1, replica_groups=mesh['bx_0'=4,'bx_1'=2,'by_0'=2,'by_1'=4,'by_2'=2] {'by_2'}, use_global_device_ids=true, to_apply=%add.9 | all-reduce | flops 2 | bytes 16 | tf_op jit(solution)/shard_map/while
  825.4 6.0 all-reduce.25
  850.0 5.7 all-reduce.28
  858.6 9.0 all-reduce.29
  881.4 8.9 all-reduce.30
  892.3 5.3 all-reduce.31
  906.5 7.7 all-reduce.33
  916.3 11.4 %all-reduce.34 = f32[2]{0:T(128)S(1)} all-reduce(f32[2]{0:T(128)S(1)} %dynamic-update-slice.34), channel_id=1, replica_groups=mesh['bx_0'=4,'bx_1'=2,'by_0'=2,'by_1'=4,'by_2'=2] {'by_2'}, use_global_device_ids=true, to_apply=%add.9 | all-reduce | flops 2 | bytes 16 | tf_op jit(solution)/shard_map/while
  (829 shorter events, 506.5 us)
Async XLA Ops:
  0.9 13.2 %copy-start.18 = (u32[128]{0:T(128)S(1)}, u32[128]{0:T(128)}, u32[]{:S(2)}) copy-start(u32[128]{0:T(128)} %constant.414) | copy-start | bytes 1540
  0.9 21.1 %copy-start.20 = (u32[128]{0:T(128)S(1)}, u32[128]{0:T(128)}, u32[]{:S(2)}) copy-start(u32[128]{0:T(128)} %constant.419) | copy-start | bytes 1540
  0.9 27.5 %copy-start.22 = (u32[128]{0:T(128)S(1)}, u32[128]{0:T(128)}, u32[]{:S(2)}) copy-start(u32[128]{0:T(128)} %constant.424) | copy-start | bytes 1540
  0.9 37.1 %copy-start.24 = (u32[128]{0:T(128)S(1)}, u32[128]{0:T(128)}, u32[]{:S(2)}) copy-start(u32[128]{0:T(128)} %constant.429) | copy-start | bytes 1540
  0.9 48.8 %copy-start.11 = (s32[12]{0:T(128)S(1)}, s32[12]{0:T(128)}, u32[]{:S(2)}) copy-start(s32[12]{0:T(128)} %param.17) | copy-start | bytes 148
  0.9 48.8 %copy-start.13 = (s32[12]{0:T(128)S(1)}, s32[12]{0:T(128)}, u32[]{:S(2)}) copy-start(s32[12]{0:T(128)} %param.18) | copy-start | bytes 148
  56.3 21.8 %collective-permute-start.1 = (f32[3,1,15,128]{3,2,1,0:T(8,128)}, f32[3,1,15,128]{3,2,1,0:T(8,128)}, u32[]{:S(2)}, u32[]{:S(2)}) collective-permute-start(f32[3,1,15,128]{3,2,1,0:T(8,128)} %pad_maximum_fusion.23), channel_id=1, source_target_pairs={{0,112},{16,0},{32,16},{48,32},{64,48},{80,64},{96,80},{112,96},{1... | collective-permute-start | bytes 69128 | tf_op jit(solution)/shard_map/while/body/eval_jaxpr/ppermute | solution.py:26
  58.1 20.8 %collective-permute-start = (f32[3,1,15,128]{3,2,1,0:T(8,128)}, f32[3,1,15,128]{3,2,1,0:T(8,128)}, u32[]{:S(2)}, u32[]{:S(2)}) collective-permute-start(f32[3,1,15,128]{3,2,1,0:T(8,128)} %pad_maximum_fusion.22), channel_id=1, source_target_pairs={{0,16},{16,32},{32,48},{48,64},{64,80},{80,96},{96,112},{112,0},{1... | collective-permute-start | bytes 69128 | tf_op jit(solution)/shard_map/while/body/eval_jaxpr/ppermute | solution.py:26
  82.5 54.8 %copy-start.1 = (f32[15,15,128]{2,1,0:T(8,128)S(1)}, f32[15,15,128]{2,1,0:T(8,128)}, u32[]{:S(2)}) copy-start(f32[15,15,128]{2,1,0:T(8,128)} %get-tuple-element.553) | copy-start | bytes 345604 | tf_op jit(solution)/shard_map/while
  82.5 54.8 %copy-start.2 = (f32[15,15,128]{2,1,0:T(8,128)S(1)}, f32[15,15,128]{2,1,0:T(8,128)}, u32[]{:S(2)}) copy-start(f32[15,15,128]{2,1,0:T(8,128)} %get-tuple-element.561) | copy-start | bytes 345604 | tf_op jit(solution)/shard_map/while
  82.5 54.8 %copy-start.3 = (f32[15,15,128]{2,1,0:T(8,128)S(1)}, f32[15,15,128]{2,1,0:T(8,128)}, u32[]{:S(2)}) copy-start(f32[15,15,128]{2,1,0:T(8,128)} %get-tuple-element.556) | copy-start | bytes 345604 | tf_op jit(solution)/shard_map/while
  141.3 3.4 collective-permute-start.3
  141.7 2.9 collective-permute-start.2
  206.0 21.8 %collective-permute-start.1 = (f32[3,1,15,128]{3,2,1,0:T(8,128)}, f32[3,1,15,128]{3,2,1,0:T(8,128)}, u32[]{:S(2)}, u32[]{:S(2)}) collective-permute-start(f32[3,1,15,128]{3,2,1,0:T(8,128)} %pad_maximum_fusion.23), channel_id=1, source_target_pairs={{0,112},{16,0},{32,16},{48,32},{64,48},{80,64},{96,80},{112,96},{1... | collective-permute-start | bytes 69128 | tf_op jit(solution)/shard_map/while/body/eval_jaxpr/ppermute | solution.py:26
  207.0 21.6 %collective-permute-start = (f32[3,1,15,128]{3,2,1,0:T(8,128)}, f32[3,1,15,128]{3,2,1,0:T(8,128)}, u32[]{:S(2)}, u32[]{:S(2)}) collective-permute-start(f32[3,1,15,128]{3,2,1,0:T(8,128)} %pad_maximum_fusion.22), channel_id=1, source_target_pairs={{0,16},{16,32},{32,48},{48,64},{64,80},{80,96},{96,112},{112,0},{1... | collective-permute-start | bytes 69128 | tf_op jit(solution)/shard_map/while/body/eval_jaxpr/ppermute | solution.py:26
  232.2 50.5 %copy-start.1 = (f32[15,15,128]{2,1,0:T(8,128)S(1)}, f32[15,15,128]{2,1,0:T(8,128)}, u32[]{:S(2)}) copy-start(f32[15,15,128]{2,1,0:T(8,128)} %get-tuple-element.553) | copy-start | bytes 345604 | tf_op jit(solution)/shard_map/while
  232.2 50.5 %copy-start.2 = (f32[15,15,128]{2,1,0:T(8,128)S(1)}, f32[15,15,128]{2,1,0:T(8,128)}, u32[]{:S(2)}) copy-start(f32[15,15,128]{2,1,0:T(8,128)} %get-tuple-element.561) | copy-start | bytes 345604 | tf_op jit(solution)/shard_map/while
  232.2 50.5 %copy-start.3 = (f32[15,15,128]{2,1,0:T(8,128)S(1)}, f32[15,15,128]{2,1,0:T(8,128)}, u32[]{:S(2)}) copy-start(f32[15,15,128]{2,1,0:T(8,128)} %get-tuple-element.556) | copy-start | bytes 345604 | tf_op jit(solution)/shard_map/while
  286.7 3.3 collective-permute-start.3
  287.2 2.9 collective-permute-start.2
  353.1 21.8 %collective-permute-start.1 = (f32[3,1,15,128]{3,2,1,0:T(8,128)}, f32[3,1,15,128]{3,2,1,0:T(8,128)}, u32[]{:S(2)}, u32[]{:S(2)}) collective-permute-start(f32[3,1,15,128]{3,2,1,0:T(8,128)} %pad_maximum_fusion.23), channel_id=1, source_target_pairs={{0,112},{16,0},{32,16},{48,32},{64,48},{80,64},{96,80},{112,96},{1... | collective-permute-start | bytes 69128 | tf_op jit(solution)/shard_map/while/body/eval_jaxpr/ppermute | solution.py:26
  354.0 21.6 %collective-permute-start = (f32[3,1,15,128]{3,2,1,0:T(8,128)}, f32[3,1,15,128]{3,2,1,0:T(8,128)}, u32[]{:S(2)}, u32[]{:S(2)}) collective-permute-start(f32[3,1,15,128]{3,2,1,0:T(8,128)} %pad_maximum_fusion.22), channel_id=1, source_target_pairs={{0,16},{16,32},{32,48},{48,64},{64,80},{80,96},{96,112},{112,0},{1... | collective-permute-start | bytes 69128 | tf_op jit(solution)/shard_map/while/body/eval_jaxpr/ppermute | solution.py:26
  379.2 49.5 %copy-start.1 = (f32[15,15,128]{2,1,0:T(8,128)S(1)}, f32[15,15,128]{2,1,0:T(8,128)}, u32[]{:S(2)}) copy-start(f32[15,15,128]{2,1,0:T(8,128)} %get-tuple-element.553) | copy-start | bytes 345604 | tf_op jit(solution)/shard_map/while
  379.2 49.5 %copy-start.2 = (f32[15,15,128]{2,1,0:T(8,128)S(1)}, f32[15,15,128]{2,1,0:T(8,128)}, u32[]{:S(2)}) copy-start(f32[15,15,128]{2,1,0:T(8,128)} %get-tuple-element.561) | copy-start | bytes 345604 | tf_op jit(solution)/shard_map/while
  379.2 49.5 %copy-start.3 = (f32[15,15,128]{2,1,0:T(8,128)S(1)}, f32[15,15,128]{2,1,0:T(8,128)}, u32[]{:S(2)}) copy-start(f32[15,15,128]{2,1,0:T(8,128)} %get-tuple-element.556) | copy-start | bytes 345604 | tf_op jit(solution)/shard_map/while
  432.7 3.3 collective-permute-start.3
  433.2 2.9 collective-permute-start.2
  499.8 21.8 %collective-permute-start.1 = (f32[3,1,15,128]{3,2,1,0:T(8,128)}, f32[3,1,15,128]{3,2,1,0:T(8,128)}, u32[]{:S(2)}, u32[]{:S(2)}) collective-permute-start(f32[3,1,15,128]{3,2,1,0:T(8,128)} %pad_maximum_fusion.23), channel_id=1, source_target_pairs={{0,112},{16,0},{32,16},{48,32},{64,48},{80,64},{96,80},{112,96},{1... | collective-permute-start | bytes 69128 | tf_op jit(solution)/shard_map/while/body/eval_jaxpr/ppermute | solution.py:26
  500.7 21.6 %collective-permute-start = (f32[3,1,15,128]{3,2,1,0:T(8,128)}, f32[3,1,15,128]{3,2,1,0:T(8,128)}, u32[]{:S(2)}, u32[]{:S(2)}) collective-permute-start(f32[3,1,15,128]{3,2,1,0:T(8,128)} %pad_maximum_fusion.22), channel_id=1, source_target_pairs={{0,16},{16,32},{32,48},{48,64},{64,80},{80,96},{96,112},{112,0},{1... | collective-permute-start | bytes 69128 | tf_op jit(solution)/shard_map/while/body/eval_jaxpr/ppermute | solution.py:26
  525.9 49.5 %copy-start.1 = (f32[15,15,128]{2,1,0:T(8,128)S(1)}, f32[15,15,128]{2,1,0:T(8,128)}, u32[]{:S(2)}) copy-start(f32[15,15,128]{2,1,0:T(8,128)} %get-tuple-element.553) | copy-start | bytes 345604 | tf_op jit(solution)/shard_map/while
  525.9 49.5 %copy-start.2 = (f32[15,15,128]{2,1,0:T(8,128)S(1)}, f32[15,15,128]{2,1,0:T(8,128)}, u32[]{:S(2)}) copy-start(f32[15,15,128]{2,1,0:T(8,128)} %get-tuple-element.561) | copy-start | bytes 345604 | tf_op jit(solution)/shard_map/while
  525.9 49.5 %copy-start.3 = (f32[15,15,128]{2,1,0:T(8,128)S(1)}, f32[15,15,128]{2,1,0:T(8,128)}, u32[]{:S(2)}) copy-start(f32[15,15,128]{2,1,0:T(8,128)} %get-tuple-element.556) | copy-start | bytes 345604 | tf_op jit(solution)/shard_map/while
  579.4 3.3 collective-permute-start.3
  579.8 2.9 collective-permute-start.2
  646.8 21.8 %collective-permute-start.1 = (f32[3,1,15,128]{3,2,1,0:T(8,128)}, f32[3,1,15,128]{3,2,1,0:T(8,128)}, u32[]{:S(2)}, u32[]{:S(2)}) collective-permute-start(f32[3,1,15,128]{3,2,1,0:T(8,128)} %pad_maximum_fusion.23), channel_id=1, source_target_pairs={{0,112},{16,0},{32,16},{48,32},{64,48},{80,64},{96,80},{112,96},{1... | collective-permute-start | bytes 69128 | tf_op jit(solution)/shard_map/while/body/eval_jaxpr/ppermute | solution.py:26
  647.7 21.6 %collective-permute-start = (f32[3,1,15,128]{3,2,1,0:T(8,128)}, f32[3,1,15,128]{3,2,1,0:T(8,128)}, u32[]{:S(2)}, u32[]{:S(2)}) collective-permute-start(f32[3,1,15,128]{3,2,1,0:T(8,128)} %pad_maximum_fusion.22), channel_id=1, source_target_pairs={{0,16},{16,32},{32,48},{48,64},{64,80},{80,96},{96,112},{112,0},{1... | collective-permute-start | bytes 69128 | tf_op jit(solution)/shard_map/while/body/eval_jaxpr/ppermute | solution.py:26
  673.0 49.5 %copy-start.1 = (f32[15,15,128]{2,1,0:T(8,128)S(1)}, f32[15,15,128]{2,1,0:T(8,128)}, u32[]{:S(2)}) copy-start(f32[15,15,128]{2,1,0:T(8,128)} %get-tuple-element.553) | copy-start | bytes 345604 | tf_op jit(solution)/shard_map/while
  673.0 49.5 %copy-start.2 = (f32[15,15,128]{2,1,0:T(8,128)S(1)}, f32[15,15,128]{2,1,0:T(8,128)}, u32[]{:S(2)}) copy-start(f32[15,15,128]{2,1,0:T(8,128)} %get-tuple-element.561) | copy-start | bytes 345604 | tf_op jit(solution)/shard_map/while
  673.0 49.5 %copy-start.3 = (f32[15,15,128]{2,1,0:T(8,128)S(1)}, f32[15,15,128]{2,1,0:T(8,128)}, u32[]{:S(2)}) copy-start(f32[15,15,128]{2,1,0:T(8,128)} %get-tuple-element.556) | copy-start | bytes 345604 | tf_op jit(solution)/shard_map/while
  726.5 3.3 collective-permute-start.3
  726.9 2.9 collective-permute-start.2
  793.5 21.8 %collective-permute-start.1 = (f32[3,1,15,128]{3,2,1,0:T(8,128)}, f32[3,1,15,128]{3,2,1,0:T(8,128)}, u32[]{:S(2)}, u32[]{:S(2)}) collective-permute-start(f32[3,1,15,128]{3,2,1,0:T(8,128)} %pad_maximum_fusion.23), channel_id=1, source_target_pairs={{0,112},{16,0},{32,16},{48,32},{64,48},{80,64},{96,80},{112,96},{1... | collective-permute-start | bytes 69128 | tf_op jit(solution)/shard_map/while/body/eval_jaxpr/ppermute | solution.py:26
  794.4 21.6 %collective-permute-start = (f32[3,1,15,128]{3,2,1,0:T(8,128)}, f32[3,1,15,128]{3,2,1,0:T(8,128)}, u32[]{:S(2)}, u32[]{:S(2)}) collective-permute-start(f32[3,1,15,128]{3,2,1,0:T(8,128)} %pad_maximum_fusion.22), channel_id=1, source_target_pairs={{0,16},{16,32},{32,48},{48,64},{64,80},{80,96},{96,112},{112,0},{1... | collective-permute-start | bytes 69128 | tf_op jit(solution)/shard_map/while/body/eval_jaxpr/ppermute | solution.py:26
  819.6 49.5 %copy-start.1 = (f32[15,15,128]{2,1,0:T(8,128)S(1)}, f32[15,15,128]{2,1,0:T(8,128)}, u32[]{:S(2)}) copy-start(f32[15,15,128]{2,1,0:T(8,128)} %get-tuple-element.553) | copy-start | bytes 345604 | tf_op jit(solution)/shard_map/while
  819.6 49.5 %copy-start.2 = (f32[15,15,128]{2,1,0:T(8,128)S(1)}, f32[15,15,128]{2,1,0:T(8,128)}, u32[]{:S(2)}) copy-start(f32[15,15,128]{2,1,0:T(8,128)} %get-tuple-element.561) | copy-start | bytes 345604 | tf_op jit(solution)/shard_map/while
  819.6 49.5 %copy-start.3 = (f32[15,15,128]{2,1,0:T(8,128)S(1)}, f32[15,15,128]{2,1,0:T(8,128)}, u32[]{:S(2)}) copy-start(f32[15,15,128]{2,1,0:T(8,128)} %get-tuple-element.556) | copy-start | bytes 345604 | tf_op jit(solution)/shard_map/while
  873.1 3.3 collective-permute-start.3
  873.6 2.9 collective-permute-start.2
  (97 other events, 422.6 us)
